TPU v7x, 512 devices: a whole 4x4x16 slice. The times are simulated.
512 devices in a mesh: grp: 64 (over y, z_hi, x, core), node: 8 (over z_lo).
Axes of the slice: x: 4, y: 4, z: 16 (z_hi: 2, z_lo: 8; z = z_hi * 8 + z_lo), core: 2. Of those that a mesh axis runs over, the one named last changes fastest.
Arguments:
- grad_out: bfloat16 [24576, 2048], P('grp', 'node'), may hold values from -32 to 32
- gate_prob: float32 [24576], P('grp'), may hold values from 0.05 to 1
- hidden: bfloat16 [24576, 7168], P('grp', 'node'), may hold values from -0.19921875 to 0.19921875
- w_down: bfloat16 [2048, 7168], P(None, 'node'), may hold values from -0.0625 to 0.0625
- slot_counts: int32 [64], P('grp'), may hold values from 0 to 384, as said below
Outputs:
- grad_hidden: bfloat16 [24576, 7168], P('grp', 'node')
- grad_weight: bfloat16 [2048, 7168], P('grp', 'node')
Inputs may be any that keep to these rules, and one draw needn't show every extreme that they name: `slot_counts`: each count is a multiple of 128; in every draw some group's count is 384.
All inputs are finite; a program needn't handle non-finite values.
Results may differ from a plain program's by a relative error of at most 0.0057.
Values may be sent and summed in bfloat16 or wider, within the bound.
No kernel may reach another device: no remote copies, remote signals or barrier semaphores. Data moves between devices by JAX's collectives and lax.ppermute only.
A program may use at most 64 MiB of HBM per device.

v0:
```python
import jax
import jax.numpy as jnp
from jax import lax
from jax.sharding import PartitionSpec as P

TILE_ROWS = 128


def hidden_grads(features, w_down, tile_rows, first_tile, tile_count):
    buffer_rows = features.shape[0]
    zeros_out = jnp.zeros((buffer_rows, w_down.shape[1]), jnp.bfloat16)

    def hidden_one_tile(tile_index, result):
        tile_block = lax.dynamic_slice_in_dim(features, tile_index * tile_rows, tile_rows, 0)
        product = jnp.dot(tile_block, w_down, preferred_element_type=jnp.float32).astype(
            jnp.bfloat16
        )
        return lax.dynamic_update_slice_in_dim(result, product, tile_index * tile_rows, 0)

    return lax.fori_loop(first_tile, first_tile + tile_count, hidden_one_tile, zeros_out)


def weight_term(features, hidden_part, tile_rows, tile_count):

    def weight_one_tile(tile_index, running):
        slot_block = lax.dynamic_slice_in_dim(features, tile_index * tile_rows, tile_rows, 0)
        unit_block = lax.dynamic_slice_in_dim(hidden_part, tile_index * tile_rows, tile_rows, 0)
        return running + lax.dot_general(
            slot_block, unit_block, (((0,), (0,)), ((), ())), preferred_element_type=jnp.float32
        )

    start_sum = jnp.zeros((features.shape[1], hidden_part.shape[1]), jnp.float32)
    return lax.fori_loop(0, tile_count, weight_one_tile, start_sum)


def owner_rows(received):
    return jnp.sum(received.astype(jnp.float32), axis=0)


def body(grad_out, gate_prob, hidden, w_down, slot_counts):
    tile_rows = TILE_ROWS
    own_tiles = slot_counts[0] // tile_rows
    scaled = (gate_prob[:, None] * grad_out.astype(jnp.float32)).astype(jnp.bfloat16)
    gathered = lax.all_gather(scaled, "node", axis=1, tiled=True)
    grad_hidden = hidden_grads(gathered, w_down, tile_rows, 0, own_tiles)
    group_count = lax.axis_size("grp")
    model_rows = gathered.shape[1]
    rows_here = model_rows // group_count
    whole_term = weight_term(gathered, hidden, tile_rows, own_tiles).astype(jnp.bfloat16)
    blocks = whole_term.reshape(group_count, rows_here, hidden.shape[1])
    received = lax.all_to_all(blocks, "grp", split_axis=0, concat_axis=0, tiled=True)
    summed = owner_rows(received)
    return (grad_hidden, summed.astype(jnp.bfloat16))


def solution(mesh):
    return jax.shard_map(
        body,
        mesh=mesh,
        in_specs=(P("grp", "node"), P("grp"), P("grp", "node"), P(None, "node"), P("grp")),
        out_specs=(P("grp", "node"), P("grp", "node")),
        check_vma=False,
    )
```

profile of v0, /device:TPU:97, one launch (start us, length us, event | category | flops | bytes accessed | tf_op | source)
XLA Modules:
  0.0 307.5 jit_solution(12469548475492476656)
XLA Ops:
  7.2 0.0 all-gather.2.cloned.1.call-start
  7.2 1.7 multiply_convert_fusion
  8.9 0.0 all-gather.2.cloned.1.call-update
  9.6 61.6 %all-gather.2.cloned.1.call-done = bf16[384,2048]{1,0:T(8,128)(2,1)} async-done(((bf16[384,256]{1,0:T(8,128)(2,1)}), bf16[384,2048]{1,0:T(8,128)(2,1)}) %all-gather.2.cloned.1.call-update) | async-done | bytes 1572880 | tf_op jit(solution)/shard_map/all_gather | solution.py:44
  71.2 0.0 copy-start
  71.2 3.4 %broadcast_in_dim.8 = f32[2048,896]{1,0:T(8,128)} broadcast(f32[]{:T(128)} %constant.38.clone.1), dimensions={} | broadcast | bytes 7340036 | tf_op jit(solution)/shard_map/broadcast_in_dim | solution.py:32
  74.6 0.0 copy-done
  74.6 7.3 %while.21 = (s32[]{:T(128)}, f32[2048,896]{1,0:T(8,128)}, s32[]{:T(128)}, bf16[384,2048]{1,0:T(8,128)(2,1)S(1)}, bf16[384,896]{1,0:T(8,128)(2,1)}, /*index=5*/s32[]{:T(128)}, s32[]{:T(128)}, s32[]{:T(128)}, s32[]{:T(128)}) while((s32[]{:T(128)}, f32[2048,896]{1,0:T(8,128)}, s32[]{:T(128)}, bf16[384,2048]{1,0:T(8,128)(2,1)S(1)}, ...), condition=%wide.region_3.4_spmd, body=%wide.region_2.3_spmd.sunk | while | flops 471597056 | bytes 15434891 | solution.py:33
  74.7 7.3 %convolution_add_fusion.2 = f32[2048,896]{1,0:T(8,128)} fusion(f32[2048,896]{1,0:T(8,128)} %get-tuple-element.181, bf16[384,2048]{1,0:T(8,128)(2,1)S(1)} %get-tuple-element.192, s32[]{:T(128)S(6)} %select_n.17, bf16[384,896]{1,0:T(8,128)(2,1)} %get-tuple-element.193), kind=kOutput, calls=%fused_computation.4.clone.1 | convolution fusion | flops 471597056 | bytes 15434752 | tf_op jit(solution)/shard_map/while/body/dot_general | solution.py:28
  82.0 5.4 %convert_element_type.16 = bf16[2048,896]{1,0:T(8,128)(2,1)} convert(f32[2048,896]{1,0:T(8,128)} %get-tuple-element.59) | non-fusion elementwise | flops 1835008 | bytes 11010048 | tf_op jit(solution)/shard_map/convert_element_type | solution.py:49
  87.4 30.0 %all-to-all-start = ((bf16[64,32,896]{2,1,0:T(8,128)(2,1)}), bf16[64,32,896]{2,1,0:T(8,128)(2,1)}, u32[]{:S(2)}, u32[]{:S(2)}) async-start(bf16[64,32,896]{2,1,0:T(8,128)(2,1)} %bitcast.9), calls=%async_computation | async-start | bytes 7340032 | tf_op jit(solution)/shard_map/all_to_all | solution.py:51
  117.4 0.1 broadcast_in_dim.7
  117.4 2.8 while.20
  117.5 2.8 fusion.14
  120.2 0.0 copy-start.1
  120.3 177.2 %all-to-all-done = bf16[64,32,896]{2,1,0:T(8,128)(2,1)} async-done(((bf16[64,32,896]{2,1,0:T(8,128)(2,1)}), bf16[64,32,896]{2,1,0:T(8,128)(2,1)}, u32[]{:S(2)}, u32[]{:S(2)}) %all-to-all-start) | async-done | bytes 3670048 | tf_op jit(solution)/shard_map/all_to_all | solution.py:51
  297.4 3.2 %reduce_sum.12 = bf16[32,896]{1,0:T(8,128)(2,1)} reduce(bf16[64,32,896]{2,1,0:T(8,128)(2,1)} %all-to-all-done, bf16[]{:T(256)} %constant.33.clone.1), dimensions={0}, to_apply=%region_4.5 | reduce | flops 1806336 | bytes 3727362 | tf_op jit(solution)/shard_map/reduce_sum | solution.py:37
  300.6 0.0 copy-done.1
Async XLA Ops:
  7.2 64.1 %all-gather.2.cloned.1.call-start = ((), (), s32[]{:S(2)}) async-start(), calls=%async_computation.1 | async-start | bytes 1769472 | tf_op jit(solution)/shard_map/all_gather | solution.py:44
  71.2 3.4 %copy-start = (bf16[384,2048]{1,0:T(8,128)(2,1)S(1)}, bf16[384,2048]{1,0:T(8,128)(2,1)}, u32[]{:S(2)}) copy-start(bf16[384,2048]{1,0:T(8,128)(2,1)} %all-gather.2.cloned.1.call-done) | copy-start | bytes 4718596
  87.4 210.1 %all-to-all-start = ((bf16[64,32,896]{2,1,0:T(8,128)(2,1)}), bf16[64,32,896]{2,1,0:T(8,128)(2,1)}, u32[]{:S(2)}, u32[]{:S(2)}) async-start(bf16[64,32,896]{2,1,0:T(8,128)(2,1)} %bitcast.9), calls=%async_computation | async-start | bytes 7340032 | tf_op jit(solution)/shard_map/all_to_all | solution.py:51
  120.2 180.4 %copy-start.1 = (bf16[384,896]{1,0:T(8,128)(2,1)}, bf16[384,896]{1,0:T(8,128)(2,1)S(1)}, u32[]{:S(2)}) copy-start(bf16[384,896]{1,0:T(8,128)(2,1)S(1)} %get-tuple-element.56) | copy-start | bytes 2064388
Sparse Core Ops, SparseCore 0:
  10.6 60.6 all-gather.1
where the time goes:
time: 308 us; the launch traced here: 307 us
  waiting for transfers between devices  239 us (78%)
  starting transfers between devices  30 us (10%)
  between operations  14.7 us (5%)
  other arithmetic  10.3 us (3%)
  matrix products  10.1 us (3%)
  local copies, waits for them, and re-layouts  3.49 us (1%)
    all_to_all x1, waiting for transfers between devices, body(): lax.all_to_all(blocks, 'grp', split_axis=0, concat_axis=0, tiled=True)  177 us
    all_gather x1, waiting for transfers between devices, body(): gathered = lax.all_gather(scaled, 'node', axis=1, tiled=True)  61.6 us
    all_to_all x1, starting transfers between devices, body(): lax.all_to_all(blocks, 'grp', split_axis=0, concat_axis=0, tiled=True)  30 us
    dot_general x1, matrix products, weight_one_tile(): lax.dot_general(slot_block, unit_block, (((0,), (0,)), ((), ())), preferr...  7.32 us
  transfers between devices with their start and end apart: 2, of which 2 were waited for; matrix products, arithmetic and copies ran while one was open for 1% of the time, Pallas kernels for 0%

commit v1 on v0

--- a/solution.py
+++ b/solution.py
@@ -1,9 +1,17 @@
+import functools
 import jax
 import jax.numpy as jnp
 from jax import lax
 from jax.sharding import PartitionSpec as P
 
 TILE_ROWS = 128
+
+
+def _lead_regions(t0, along_axis):
+    return jnp.concatenate(lax.all_gather(t0, along_axis), 1)
+
+
+set_results_by_axis = functools.partial(_lead_regions, along_axis="node")
 
 
 def hidden_grads(features, w_down, tile_rows, first_tile, tile_count):
@@ -41,7 +49,7 @@
     tile_rows = TILE_ROWS
     own_tiles = slot_counts[0] // tile_rows
     scaled = (gate_prob[:, None] * grad_out.astype(jnp.float32)).astype(jnp.bfloat16)
-    gathered = lax.all_gather(scaled, "node", axis=1, tiled=True)
+    gathered = set_results_by_axis(scaled)
     grad_hidden = hidden_grads(gathered, w_down, tile_rows, 0, own_tiles)
     group_count = lax.axis_size("grp")
     model_rows = gathered.shape[1]

time: 308 us -> 308 us (level)
  the two profiles are of different devices: /device:TPU:97 before, /device:TPU:103 now
where the time goes in v1:
time: 308 us
  waiting for transfers between devices  227 us (74%)
  matrix products  30.2 us (10%)
  starting transfers between devices  20.2 us (7%)
  between operations  14.7 us (5%)
  other arithmetic  10.3 us (3%)
  local copies, waits for them, and re-layouts  5.08 us (2%)
    all_to_all x1, waiting for transfers between devices, body(): lax.all_to_all(blocks, 'grp', split_axis=0, concat_axis=0, tiled=True)  171 us
    all_gather x1, waiting for transfers between devices, _lead_regions(): return jnp.concatenate(lax.all_gather(t0, along_axis), 1)  55.9 us
    dot_general x3, matrix products, weight_one_tile(): lax.dot_general(slot_block, unit_block, (((0,), (0,)), ((), ())), preferr...  21.9 us
    all_to_all x1, starting transfers between devices, body(): lax.all_to_all(blocks, 'grp', split_axis=0, concat_axis=0, tiled=True)  20.1 us
    dot_general x3, matrix products, hidden_one_tile(): jnp.dot(tile_block, w_down, preferred_element_type=jnp.float32)  8.32 us
  transfers between devices with their start and end apart: 2, of which 2 were waited for; matrix products, arithmetic and copies ran while one was open for 3% of the time, Pallas kernels for 0%

profile of v1, /device:TPU:103, one launch (start us, length us, event | category | flops | bytes accessed | tf_op | source)
XLA Modules:
  0.0 307.6 jit_solution(6094530446661680583)
XLA Ops:
  7.2 0.0 all-gather.3.cloned.1.call-start
  7.2 1.7 multiply_convert_fusion
  8.9 0.0 all-gather.3.cloned.1.call-update
  9.6 55.9 %all-gather.3.cloned.1.call-done = bf16[3072,256]{1,0:T(8,128)(2,1)} async-done(((bf16[384,256]{1,0:T(8,128)(2,1)}), bf16[3072,256]{1,0:T(8,128)(2,1)}) %all-gather.3.cloned.1.call-update) | async-done | bytes 1572880 | tf_op jit(solution)/shard_map/all_gather | solution.py:11
  65.5 1.6 copy.8
  67.1 3.4 %broadcast_in_dim.8 = f32[2048,896]{1,0:T(8,128)} broadcast(f32[]{:T(128)} %constant.38.clone.1), dimensions={} | broadcast | bytes 7340036 | tf_op jit(solution)/shard_map/broadcast_in_dim | solution.py:40
  70.6 21.9 %while.21 = (s32[]{:T(128)}, f32[2048,896]{1,0:T(8,128)}, s32[]{:T(128)}, bf16[384,2048]{1,0:T(8,128)(2,1)S(1)}, bf16[384,896]{1,0:T(8,128)(2,1)}, /*index=5*/s32[]{:T(128)}, s32[]{:T(128)}, s32[]{:T(128)}, s32[]{:T(128)}) while((s32[]{:T(128)}, f32[2048,896]{1,0:T(8,128)}, s32[]{:T(128)}, bf16[384,2048]{1,0:T(8,128)(2,1)S(1)}, ...), condition=%wide.region_3.4_spmd, body=%wide.region_2.3_spmd.sunk | while | flops 471597056 | bytes 15434891 | solution.py:41
  70.6 7.3 %convolution_add_fusion.2 = f32[2048,896]{1,0:T(8,128)} fusion(f32[2048,896]{1,0:T(8,128)} %get-tuple-element.181, bf16[384,2048]{1,0:T(8,128)(2,1)S(1)} %get-tuple-element.192, s32[]{:T(128)S(6)} %select_n.17, bf16[384,896]{1,0:T(8,128)(2,1)} %get-tuple-element.193), kind=kOutput, calls=%fused_computation.4.clone.1 | convolution fusion | flops 471597056 | bytes 15434752 | tf_op jit(solution)/shard_map/while/body/dot_general | solution.py:36
  77.9 7.3 %convolution_add_fusion.2 = f32[2048,896]{1,0:T(8,128)} fusion(f32[2048,896]{1,0:T(8,128)} %get-tuple-element.181, bf16[384,2048]{1,0:T(8,128)(2,1)S(1)} %get-tuple-element.192, s32[]{:T(128)S(6)} %select_n.17, bf16[384,896]{1,0:T(8,128)(2,1)} %get-tuple-element.193), kind=kOutput, calls=%fused_computation.4.clone.1 | convolution fusion | flops 471597056 | bytes 15434752 | tf_op jit(solution)/shard_map/while/body/dot_general | solution.py:36
  85.2 7.3 %convolution_add_fusion.2 = f32[2048,896]{1,0:T(8,128)} fusion(f32[2048,896]{1,0:T(8,128)} %get-tuple-element.181, bf16[384,2048]{1,0:T(8,128)(2,1)S(1)} %get-tuple-element.192, s32[]{:T(128)S(6)} %select_n.17, bf16[384,896]{1,0:T(8,128)(2,1)} %get-tuple-element.193), kind=kOutput, calls=%fused_computation.4.clone.1 | convolution fusion | flops 471597056 | bytes 15434752 | tf_op jit(solution)/shard_map/while/body/dot_general | solution.py:36
  92.5 5.4 %convert_element_type.16 = bf16[2048,896]{1,0:T(8,128)(2,1)} convert(f32[2048,896]{1,0:T(8,128)} %get-tuple-element.59) | non-fusion elementwise | flops 1835008 | bytes 11010048 | tf_op jit(solution)/shard_map/convert_element_type | solution.py:57
  97.8 20.1 %all-to-all-start = ((bf16[64,32,896]{2,1,0:T(8,128)(2,1)}), bf16[64,32,896]{2,1,0:T(8,128)(2,1)}, u32[]{:S(2)}, u32[]{:S(2)}) async-start(bf16[64,32,896]{2,1,0:T(8,128)(2,1)} %bitcast.16), calls=%async_computation | async-start | bytes 7340032 | tf_op jit(solution)/shard_map/all_to_all | solution.py:59
  118.0 0.1 broadcast_in_dim.7
  118.1 8.4 %while.20 = (s32[]{:T(128)}, bf16[384,896]{1,0:T(8,128)(2,1)S(1)}, s32[]{:T(128)}, bf16[384,2048]{1,0:T(8,128)(2,1)S(1)}, bf16[2048,896]{1,0:T(8,128)(2,1)}, /*index=5*/s32[]{:T(128)}, s32[]{:T(128)}, s32[]{:T(128)}, s32[]{:T(128)}) while((s32[]{:T(128)}, bf16[384,896]{1,0:T(8,128)(2,1)S(1)}, s32[]{:T(128)}, bf16[384,2048]{1,0:T(8,128)(2,1)S(1)}, ...), condition=%wide.region_1.2_spmd, body=%wide.region_0.1_spmd.sunk | while | flops 469876736 | bytes 4424843 | solution.py:28
  118.1 2.8 fusion.14
  120.9 2.8 fusion.14
  123.7 2.8 fusion.14
  126.5 0.0 copy-start
  126.5 171.0 %all-to-all-done = bf16[64,32,896]{2,1,0:T(8,128)(2,1)} async-done(((bf16[64,32,896]{2,1,0:T(8,128)(2,1)}), bf16[64,32,896]{2,1,0:T(8,128)(2,1)}, u32[]{:S(2)}, u32[]{:S(2)}) %all-to-all-start) | async-done | bytes 3670048 | tf_op jit(solution)/shard_map/all_to_all | solution.py:59
  297.5 3.2 %reduce_sum.12 = bf16[32,896]{1,0:T(8,128)(2,1)} reduce(bf16[64,32,896]{2,1,0:T(8,128)(2,1)} %all-to-all-done, bf16[]{:T(256)} %constant.33.clone.1), dimensions={0}, to_apply=%region_4.5 | reduce | flops 1806336 | bytes 3727362 | tf_op jit(solution)/shard_map/reduce_sum | solution.py:45
  300.7 0.0 copy-done
Async XLA Ops:
  7.2 58.4 %all-gather.3.cloned.1.call-start = ((), (), s32[]{:S(2)}) async-start(), calls=%async_computation.1 | async-start | bytes 1769472 | tf_op jit(solution)/shard_map/all_gather | solution.py:11
  97.8 199.7 %all-to-all-start = ((bf16[64,32,896]{2,1,0:T(8,128)(2,1)}), bf16[64,32,896]{2,1,0:T(8,128)(2,1)}, u32[]{:S(2)}, u32[]{:S(2)}) async-start(bf16[64,32,896]{2,1,0:T(8,128)(2,1)} %bitcast.16), calls=%async_computation | async-start | bytes 7340032 | tf_op jit(solution)/shard_map/all_to_all | solution.py:59
  126.5 174.2 %copy-start = (bf16[384,896]{1,0:T(8,128)(2,1)}, bf16[384,896]{1,0:T(8,128)(2,1)S(1)}, u32[]{:S(2)}) copy-start(bf16[384,896]{1,0:T(8,128)(2,1)S(1)} %get-tuple-element.56) | copy-start | bytes 2064388
Sparse Core Ops, SparseCore 0:
  10.6 54.8 all-gather.2
